TPU v7x, 256 devices: a whole 4x4x8 slice. The times are simulated.
256 devices in a mesh: grp: 8 (over z), ex: 32 (over y, x, core).
Axes of the slice: x: 4, y: 4, z: 8, core: 2. Of those that a mesh axis runs over, the one named last changes fastest.
Arguments:
- tokens: bfloat16 [16384, 3584], P(('grp', 'ex')), may hold values from -6 to 6
- expert_ids: int32 [16384, 8], P(('grp', 'ex')), may hold values from 0 to 127, all different within a row; in each aligned block of 64 rows (0 to 63, 64 to 127, ...) at most 5 rows name the same one
- combine: float32 [16384, 8], P(('grp', 'ex')), may hold values from 0.25 to 0.5
- hot_flags: int32 [128], replicated, may hold values from 0 to 1
- gate_up_weight: bfloat16 [8, 32, 2, 3584, 512], P('grp', 'ex'), as said below
- gate_up_scale: float32 [8, 32, 2, 28, 512], P('grp', 'ex')
- down_weight: bfloat16 [8, 32, 512, 3584], P('grp', 'ex'), as said below
- down_scale: float32 [8, 32, 4, 3584], P('grp', 'ex')
Outputs:
- moe_out: bfloat16 [16384, 3584], P(('grp', 'ex'))
Inputs may be any that keep to these rules, and one draw needn't show every extreme that they name: `expert_ids`: each row names 8 different experts; the 64 rows of one device name one expert at most 5 times. `gate_up_weight`: for an expert whose hot flag is 0, every entry is an integer from -8 to 7. `down_weight`: for an expert whose hot flag is 0, every entry is an integer from -8 to 7.
All inputs are finite; a program needn't handle non-finite values.
Results may differ from a plain program's by a relative error of at most 0.008.
Values may be sent and summed in bfloat16 or wider, within the bound.
No kernel may reach another device: no remote copies, remote signals or barrier semaphores. Data moves between devices by JAX's collectives and lax.ppermute only.
A program may use at most 128 MiB of HBM per device.

v0:
```python
import jax
import jax.numpy as jnp
from jax import lax
from jax.sharding import PartitionSpec as P


CAP = 5
HALF = 768
BOTH = 2 * HALF


def dequantize(weights, scales, is_hot):
    group_count = scales.shape[0]
    shaped = weights.reshape(group_count, weights.shape[0] // group_count, weights.shape[1])
    scaled = (shaped * scales[:, None, :]).reshape(weights.shape).astype(jnp.bfloat16)
    return jnp.where(is_hot, weights, scaled)


def matmul(a, b):
    return jnp.dot(a, b, preferred_element_type=jnp.float32)


def shards(
    tokens, expert_ids, combine, hot_flags, gate_up_weight, gate_up_scale, down_weight, down_scale
):
    group_count = lax.axis_size("grp")
    lane_count = lax.axis_size("ex")
    token_count, _ = tokens.shape
    top_count = expert_ids.shape[1]
    route_count = token_count * top_count
    block = group_count * CAP
    slot_count = lane_count * block
    column_tokens = group_count * token_count
    own_grp = lax.axis_index("grp")
    own_pair = own_grp // 2
    own_start = own_grp % 2 * HALF
    other_start = HALF - own_start
    partners = [(g, g ^ 1) for g in range(group_count)]

    flat_expert = expert_ids.reshape(route_count)
    route_order = jnp.arange(route_count, dtype=jnp.int32)
    earlier = (flat_expert[None, :] == flat_expert[:, None]) & (
        route_order[None, :] < route_order[:, None]
    )
    route_rank = jnp.sum(earlier, axis=1, dtype=jnp.int32)

    routes = jnp.concatenate(
        [
            expert_ids.astype(jnp.bfloat16),
            route_rank.reshape(token_count, top_count).astype(jnp.bfloat16),
            combine.astype(jnp.bfloat16),
        ],
        axis=1,
    )
    routes = jnp.pad(routes, ((0, 0), (0, 128 - 3 * top_count)))
    first = jnp.stack(
        [
            jnp.concatenate([tokens[:, start : start + HALF], routes], axis=1)
            for start in (0, HALF)
        ]
    )
    first = jnp.broadcast_to(first[None], (group_count // 2,) + first.shape)
    first = first.reshape(group_count, token_count, HALF + 128)
    first = lax.all_to_all(first, "grp", split_axis=0, concat_axis=0, tiled=True)
    first = first.reshape(column_tokens, HALF + 128)
    rest = lax.all_gather(tokens[:, BOTH:], "grp", axis=0, tiled=True)

    routes = first[:, HALF:]
    expert = routes[:, :top_count].astype(jnp.int32)
    rank = routes[:, top_count : 2 * top_count].astype(jnp.int32)
    weight = routes[:, 2 * top_count : 3 * top_count].astype(jnp.float32)
    source = jnp.arange(column_tokens, dtype=jnp.int32)[:, None] // token_count
    slot = (expert - own_pair * lane_count) * block + source * CAP + rank

    slots_down = lax.broadcasted_iota(jnp.int32, (slot_count, column_tokens), 0)
    slots_across = lax.broadcasted_iota(jnp.int32, (column_tokens, slot_count), 1)
    slot_t = slot.T
    pick = jnp.zeros((slot_count, column_tokens), jnp.bool_)
    mix = jnp.zeros((column_tokens, slot_count), jnp.float32)
    for k in range(top_count):
        pick = pick | (slot_t[k][None, :] == slots_down)
        mix = jnp.where(slot[:, k][:, None] == slots_across, weight[:, k][:, None], mix)
    pick = pick.astype(jnp.bfloat16)
    mix = mix.astype(jnp.bfloat16)

    is_hot = hot_flags[own_pair * lane_count + lax.axis_index("ex")] == 1
    gate_matrix = dequantize(gate_up_weight[0, 0, 0], gate_up_scale[0, 0, 0], is_hot)
    up_matrix = dequantize(gate_up_weight[0, 0, 1], gate_up_scale[0, 0, 1], is_hot)
    down_matrix = dequantize(down_weight[0, 0], down_scale[0, 0], is_hot)

    def exchange(rows):
        return lax.all_to_all(
            rows.reshape(lane_count, block, -1), "ex", split_axis=0, concat_axis=0, tiled=True
        ).reshape(slot_count, -1)

    own_rows = matmul(pick, first[:, :HALF]).astype(jnp.bfloat16)
    own_rows = exchange(own_rows)
    other_rows = lax.ppermute(own_rows, "grp", partners)
    rest_rows = matmul(pick, rest).astype(jnp.bfloat16)
    rest_rows = exchange(rest_rows)

    def project(matrix):
        return (
            matmul(own_rows, lax.dynamic_slice_in_dim(matrix, own_start, HALF, 0))
            + matmul(other_rows, lax.dynamic_slice_in_dim(matrix, other_start, HALF, 0))
            + matmul(rest_rows, matrix[BOTH:])
        )

    gate = project(gate_matrix)
    up = project(up_matrix)
    hidden = (jax.nn.silu(gate) * up).astype(jnp.bfloat16)

    rest_rows = matmul(hidden, down_matrix[:, BOTH:]).astype(jnp.bfloat16)
    rest_rows = exchange(rest_rows)
    other_rows = matmul(
        hidden, lax.dynamic_slice_in_dim(down_matrix, other_start, HALF, 1)
    ).astype(jnp.bfloat16)
    partner_rows = lax.ppermute(other_rows, "grp", partners)
    own_rows = matmul(
        hidden, lax.dynamic_slice_in_dim(down_matrix, own_start, HALF, 1)
    ).astype(jnp.bfloat16)
    own_rows = own_rows.astype(jnp.float32) + partner_rows.astype(jnp.float32)
    own_rows = own_rows.astype(jnp.bfloat16)
    own_rows = exchange(own_rows)
    rest_sums = matmul(mix, rest_rows).astype(jnp.bfloat16)
    rest_out = lax.psum_scatter(rest_sums, "grp", scatter_dimension=0, tiled=True)
    own_sums = matmul(mix, own_rows).astype(jnp.bfloat16)
    own_sums = own_sums.reshape(group_count, token_count, HALF)
    sums = lax.all_to_all(own_sums, "grp", split_axis=0, concat_axis=0, tiled=True)
    sums = sums.reshape(group_count // 2, 2, token_count, HALF).astype(jnp.float32)
    sums = jnp.sum(sums, axis=0).astype(jnp.bfloat16)
    return jnp.concatenate([sums[0], sums[1], rest_out], axis=1)


def solution(mesh):
    return jax.shard_map(
        shards,
        mesh=mesh,
        in_specs=(
            P(("grp", "ex"), None),
            P(("grp", "ex"), None),
            P(("grp", "ex"), None),
            P(),
            P("grp", "ex", None, None, None),
            P("grp", "ex", None, None, None),
            P("grp", "ex", None, None),
            P("grp", "ex", None, None),
        ),
        out_specs=P(("grp", "ex"), None),
        check_vma=False,
    )
```

profile of v0, /device:TPU:32, one launch (start us, length us, event | category | flops | bytes accessed | tf_op | source)
XLA Modules:
  0.0 332.9 jit_solution(9970790999367371088)
XLA Ops:
  9.4 1.0 fusion.49
  10.4 1.0 broadcast_in_dim.71
  11.5 8.6 %all-to-all-start = ((bf16[8,64,896]{2,1,0:T(8,128)(2,1)}), bf16[8,64,896]{2,1,0:T(8,128)(2,1)S(1)}, u32[]{:S(2)}, u32[]{:S(2)}) async-start(bf16[8,64,896]{2,1,0:T(8,128)(2,1)} %bitcast.2), calls=%async_computation | async-start | bytes 1835008 | tf_op jit(solution)/shard_map/all_to_all | solution.py:64
  20.8 27.0 %all-to-all-done = bf16[8,64,896]{2,1,0:T(8,128)(2,1)S(1)} async-done(((bf16[8,64,896]{2,1,0:T(8,128)(2,1)}), bf16[8,64,896]{2,1,0:T(8,128)(2,1)S(1)}, u32[]{:S(2)}, u32[]{:S(2)}) %all-to-all-start) | async-done | bytes 917536 | tf_op jit(solution)/shard_map/all_to_all | solution.py:64
  48.0 1.1 slice_reduce_fusion.7
  49.1 4.5 %convolution_convert_fusion.4 = bf16[1280,768]{1,0:T(8,128)(2,1)} fusion(bf16[512,896]{1,0:T(8,128)(2,1)S(1)} %bitcast.68, s32[512]{0:T(512)S(1)} %get-tuple-element.22, s32[512]{0:T(512)S(1)} %get-tuple-element.23, s32[512]{0:T(512)S(1)} %get-tuple-element.24, s32[512]{0:T(512)S(1)} %get-tuple-element.25, s32[512]{0:T(512)S(1)} %get-tuple-element.26, ...), kind=kOutput, calls=%fused_computation.16 | convolution fusion | flops 1017446400 | bytes 2768896 | tf_op jit(solution)/shard_map/dot_general | solution.py:20
  53.6 7.5 %all-to-all-start.1 = ((bf16[32,40,768]{2,1,0:T(8,128)(2,1)}), bf16[32,40,768]{2,1,0:T(8,128)(2,1)}, u32[]{:S(2)}, u32[]{:S(2)}) async-start(bf16[32,40,768]{2,1,0:T(8,128)(2,1)} %bitcast.5), calls=%async_computation.1 | async-start | bytes 3932160 | tf_op jit(solution)/shard_map/all_to_all | solution.py:92
  61.1 6.6 %all-gather.2.cloned.1.call-done = bf16[512,2048]{1,0:T(8,128)(2,1)} async-done(((bf16[64,2048]{1,0:T(8,128)(2,1)}), bf16[512,2048]{1,0:T(8,128)(2,1)}) %all-gather.2.cloned.1.call-update) | async-done | bytes 2097168 | tf_op jit(solution)/shard_map/all_gather | solution.py:66
  67.8 7.8 %convolution_convert_fusion.1 = bf16[1280,2048]{1,0:T(8,128)(2,1)} fusion(bf16[512,2048]{1,0:T(8,128)(2,1)} %all-gather.2.cloned.1.call-done, s32[512]{0:T(512)S(1)} %get-tuple-element.22, s32[512]{0:T(512)S(1)} %get-tuple-element.23, s32[512]{0:T(512)S(1)} %get-tuple-element.24, s32[512]{0:T(512)S(1)} %get-tuple-element.25, s32[512]{0:T(512)S(1)} %get-tuple-element.26, ...), kind=kOutput, calls=%fused_computation.1 | convolution fusion | flops 2696806400 | bytes 7356416 | tf_op jit(solution)/shard_map/dot_general | solution.py:20
  75.6 14.0 %all-to-all-done.1 = bf16[32,40,768]{2,1,0:T(8,128)(2,1)} async-done(((bf16[32,40,768]{2,1,0:T(8,128)(2,1)}), bf16[32,40,768]{2,1,0:T(8,128)(2,1)}, u32[]{:S(2)}, u32[]{:S(2)}) %all-to-all-start.1) | async-done | bytes 1966112 | tf_op jit(solution)/shard_map/all_to_all | solution.py:92
  89.6 5.0 %all-to-all-start.2 = ((bf16[32,40,2048]{2,1,0:T(8,128)(2,1)}), bf16[32,40,2048]{2,1,0:T(8,128)(2,1)}, u32[]{:S(2)}, u32[]{:S(2)}) async-start(bf16[32,40,2048]{2,1,0:T(8,128)(2,1)} %bitcast.64), calls=%async_computation.2 | async-start | bytes 10485760 | tf_op jit(solution)/shard_map/all_to_all | solution.py:92
  96.0 4.8 %fusion.5 = bf16[512,3584]{1,0:T(8,128)(2,1)} fusion(bf16[1,1,512,3584]{3,2,1,0:T(8,128)(2,1)} %param.14, f32[4,3584]{1,0:T(4,128)S(1)} %bitcast.74, pred[]{:T(512)} %bitcast.7), kind=kLoop, calls=%fused_computation.10 | loop fusion | flops 7340032 | bytes 7397377 | tf_op jit(solution)/shard_map/jit(_where)/select_n | solution.py:16
  100.9 4.0 %fusion.4 = (bf16[3584,512]{1,0:T(8,128)(2,1)S(1)}, bf16[3584,512]{1,0:T(8,128)(2,1)S(1)}) fusion(f32[28,512]{1,0:T(8,128)S(1)} %get-tuple-element.39, bf16[1,1,2,3584,512]{4,3,2,1,0:T(8,128)(2,1)} %param.12, pred[]{:T(512)} %bitcast.7, f32[28,512]{1,0:T(8,128)S(1)} %get-tuple-element.40), kind=kLoop, calls=%fused_computation.9 | loop fusion | flops 14680064 | bytes 14794753 | tf_op jit(solution)/shard_map/jit(_where)/select_n | solution.py:16
  105.2 4.2 %fusion.30 = f32[1280,512]{1,0:T(8,128)S(1)} fusion(bf16[1280,768]{1,0:T(8,128)(2,1)} %bitcast.6, bf16[3584,512]{1,0:T(8,128)(2,1)S(1)} %get-tuple-element.30, s32[]{:T(128)S(6)} %select_n.93), kind=kOutput, calls=%fused_computation.61 | convolution fusion | flops 1006632960 | bytes 5373956 | tf_op jit(solution)/shard_map/dot_general | solution.py:20
  109.5 4.3 %fusion.27 = f32[1280,512]{1,0:T(8,128)} fusion(bf16[1280,768]{1,0:T(8,128)(2,1)} %bitcast.6, bf16[3584,512]{1,0:T(8,128)(2,1)S(1)} %get-tuple-element.29, s32[]{:T(128)S(6)} %select_n.93), kind=kOutput, calls=%fused_computation.58 | convolution fusion | flops 1006632960 | bytes 5373956 | tf_op jit(solution)/shard_map/dot_general | solution.py:20
  113.7 46.8 %all-to-all-done.2 = bf16[32,40,2048]{2,1,0:T(8,128)(2,1)} async-done(((bf16[32,40,2048]{2,1,0:T(8,128)(2,1)}), bf16[32,40,2048]{2,1,0:T(8,128)(2,1)}, u32[]{:S(2)}, u32[]{:S(2)}) %all-to-all-start.2) | async-done | bytes 5242912 | tf_op jit(solution)/shard_map/all_to_all | solution.py:92
  160.5 5.6 %fusion.18 = f32[1280,512]{1,0:T(8,128)S(1)} fusion(bf16[1280,2048]{1,0:T(8,128)(2,1)} %bitcast.12, bf16[3584,512]{1,0:T(8,128)(2,1)} %copy-done), kind=kOutput, calls=%fused_computation.48 | convolution fusion | flops 2684354560 | bytes 9961472 | tf_op jit(solution)/shard_map/dot_general | solution.py:20
  166.1 4.8 %fusion.16 = f32[1280,512]{1,0:T(8,128)S(1)} fusion(bf16[1280,2048]{1,0:T(8,128)(2,1)} %bitcast.12, bf16[3584,512]{1,0:T(8,128)(2,1)S(1)} %copy-done.3), kind=kOutput, calls=%fused_computation.46 | convolution fusion | flops 2684354560 | bytes 9961472 | tf_op jit(solution)/shard_map/dot_general | solution.py:20
  171.0 3.3 fusion.6
  174.3 3.5 %multiply_convert_fusion = bf16[1280,512]{1,0:T(8,128)(2,1)S(1)} fusion(f32[1280,512]{1,0:T(8,128)S(1)} %fusion.6, f32[1280,512]{1,0:T(8,128)S(1)} %fusion.16, f32[1280,512]{1,0:T(8,128)S(1)} %copy-done.8, bf16[1280,768]{1,0:T(8,128)(2,1)} %collective-permute-done, bf16[3584,512]{1,0:T(8,128)(2,1)S(1)} %copy-done.3, s32[]{:T(128)S(6)} %select_n.94), kind=kOutput, calls=%fused_computation.20 | convolution fusion | flops 1011875840 | bytes 11927556 | tf_op jit(solution)/shard_map/dot_general | solution.py:20
  177.8 4.7 %convolution_convert_fusion = bf16[1280,2048]{1,0:T(8,128)(2,1)} fusion(bf16[1280,512]{1,0:T(8,128)(2,1)S(1)} %multiply_convert_fusion, bf16[512,3584]{1,0:T(8,128)(2,1)S(1)} %copy-done.1), kind=kOutput, calls=%fused_computation | convolution fusion | flops 2686976000 | bytes 8650752 | tf_op jit(solution)/shard_map/dot_general | solution.py:20
  182.5 4.9 %all-to-all-start.5 = ((bf16[32,40,2048]{2,1,0:T(8,128)(2,1)}), bf16[32,40,2048]{2,1,0:T(8,128)(2,1)}, u32[]{:S(2)}, u32[]{:S(2)}) async-start(bf16[32,40,2048]{2,1,0:T(8,128)(2,1)} %bitcast.65), calls=%async_computation.5 | async-start | bytes 10485760 | tf_op jit(solution)/shard_map/all_to_all | solution.py:92
  187.4 3.6 %convolution_convert_fusion.2 = bf16[1280,768]{1,0:T(8,128)(2,1)} fusion(bf16[1280,512]{1,0:T(8,128)(2,1)S(1)} %multiply_convert_fusion, bf16[512,3584]{1,0:T(8,128)(2,1)} %fusion.5, s32[]{:T(128)S(6)} %select_n.94), kind=kOutput, calls=%fused_computation.14 | convolution fusion | flops 1007616000 | bytes 4063236 | tf_op jit(solution)/shard_map/dot_general | solution.py:20
  191.1 1.1 slice_reduce_fusion.22
  192.4 1.1 slice_reduce_fusion.23
  193.5 59.7 %all-to-all-done.5 = bf16[32,40,2048]{2,1,0:T(8,128)(2,1)} async-done(((bf16[32,40,2048]{2,1,0:T(8,128)(2,1)}), bf16[32,40,2048]{2,1,0:T(8,128)(2,1)}, u32[]{:S(2)}, u32[]{:S(2)}) %all-to-all-start.5) | async-done | bytes 5242912 | tf_op jit(solution)/shard_map/all_to_all | solution.py:92
  253.2 8.7 %convolution_convert_fusion.5 = bf16[512,2048]{1,0:T(8,128)(2,1)} fusion(bf16[1280,2048]{1,0:T(8,128)(2,1)} %bitcast.26, bf16[512]{0:T(512)(128)(2,1)S(1)} %get-tuple-element.14, s32[512]{0:T(512)S(1)} %get-tuple-element.6, bf16[512]{0:T(512)(128)(2,1)S(1)} %get-tuple-element.15, s32[512]{0:T(512)S(1)} %get-tuple-element.7, ...), kind=kOutput, calls=%fused_computation.19 | convolution fusion | flops 2695888896 | bytes 7364608 | tf_op jit(solution)/shard_map/dot_general | solution.py:20
  261.9 2.3 add_convert_fusion
  264.3 30.1 %all_to_all.30 = bf16[32,40,768]{2,1,0:T(8,128)(2,1)S(1)} all-to-all(bf16[32,40,768]{2,1,0:T(8,128)(2,1)S(1)} %bitcast.72), channel_id=1, replica_groups=mesh['grp'=8,'ex'=32] {'ex'}, dimensions={0} | all-to-all | bytes 3932160 | tf_op jit(solution)/shard_map/all_to_all | solution.py:92
  294.4 3.9 %convolution_convert_fusion.6 = bf16[512,768]{1,0:T(8,128)(2,1)S(1)} fusion(bf16[1280,768]{1,0:T(8,128)(2,1)S(1)} %bitcast.71, bf16[512]{0:T(512)(128)(2,1)S(1)} %get-tuple-element.14, s32[512]{0:T(512)S(1)} %get-tuple-element.6, bf16[512]{0:T(512)(128)(2,1)S(1)} %get-tuple-element.15, s32[512]{0:T(512)S(1)} %get-tuple-element.7, ...), kind=kOutput, calls=%fused_computation.50 | convolution fusion | flops 1017511936 | bytes 2777088 | tf_op jit(solution)/shard_map/dot_general | solution.py:20
  298.3 25.8 %all_to_all.31 = bf16[8,64,768]{2,1,0:T(8,128)(2,1)S(1)} all-to-all(bf16[8,64,768]{2,1,0:T(8,128)(2,1)S(1)} %bitcast.73), channel_id=1, replica_groups=mesh['grp'=8,'ex'=32] {'grp'}, dimensions={0} | all-to-all | bytes 1572864 | tf_op jit(solution)/shard_map/all_to_all | solution.py:129
  324.3 1.7 pad_maximum_fusion
  (53 shorter events, 5.3 us)
Async XLA Ops:
  6.5 13.5 %copy-start.4 = (bf16[64,3584]{1,0:T(8,128)(2,1)S(1)}, bf16[64,3584]{1,0:T(8,128)(2,1)}, u32[]{:S(2)}) copy-start(bf16[64,3584]{1,0:T(8,128)(2,1)} %param.8) | copy-start | bytes 1376260
  11.5 36.3 %all-to-all-start = ((bf16[8,64,896]{2,1,0:T(8,128)(2,1)}), bf16[8,64,896]{2,1,0:T(8,128)(2,1)S(1)}, u32[]{:S(2)}, u32[]{:S(2)}) async-start(bf16[8,64,896]{2,1,0:T(8,128)(2,1)} %bitcast.2), calls=%async_computation | async-start | bytes 1835008 | tf_op jit(solution)/shard_map/all_to_all | solution.py:64
  20.0 47.8 %all-gather.2.cloned.1.call-start = ((), (), s32[]{:S(2)}) async-start(), calls=%async_computation.7 | async-start | bytes 2359296 | tf_op jit(solution)/shard_map/all_gather | solution.py:66
  53.6 36.0 %all-to-all-start.1 = ((bf16[32,40,768]{2,1,0:T(8,128)(2,1)}), bf16[32,40,768]{2,1,0:T(8,128)(2,1)}, u32[]{:S(2)}, u32[]{:S(2)}) async-start(bf16[32,40,768]{2,1,0:T(8,128)(2,1)} %bitcast.5), calls=%async_computation.1 | async-start | bytes 3932160 | tf_op jit(solution)/shard_map/all_to_all | solution.py:92
  89.6 5.0 %copy-start.7 = (s32[128]{0:T(128)S(1)}, s32[128]{0:T(128)}, u32[]{:S(2)}) copy-start(s32[128]{0:T(128)} %param.11) | copy-start | bytes 1540
  89.6 6.3 %copy-start.6 = (f32[1,1,4,3584]{3,2,1,0:T(4,128)S(1)}, f32[1,1,4,3584]{3,2,1,0:T(4,128)}, u32[]{:S(2)}) copy-start(f32[1,1,4,3584]{3,2,1,0:T(4,128)} %param.15) | copy-start | bytes 172036
  89.6 70.9 %all-to-all-start.2 = ((bf16[32,40,2048]{2,1,0:T(8,128)(2,1)}), bf16[32,40,2048]{2,1,0:T(8,128)(2,1)}, u32[]{:S(2)}, u32[]{:S(2)}) async-start(bf16[32,40,2048]{2,1,0:T(8,128)(2,1)} %bitcast.64), calls=%async_computation.2 | async-start | bytes 10485760 | tf_op jit(solution)/shard_map/all_to_all | solution.py:92
  95.9 4.8 %copy-start.5 = (f32[1,1,2,28,512]{4,2,3,1,0:T(2,128)S(1)}, f32[1,1,2,28,512]{4,2,3,1,0:T(2,128)}, u32[]{:S(2)}) copy-start(f32[1,1,2,28,512]{4,2,3,1,0:T(2,128)} %param.13) | copy-start | bytes 344068
  104.9 4.5 %copy-start = (bf16[3584,512]{1,0:T(8,128)(2,1)}, bf16[3584,512]{1,0:T(8,128)(2,1)S(1)}, u32[]{:S(2)}) copy-start(bf16[3584,512]{1,0:T(8,128)(2,1)S(1)} %get-tuple-element.30) | copy-start | bytes 11010052
  104.9 4.5 %copy-start.2 = (bf16[3584,512]{1,0:T(8,128)(2,1)}, bf16[3584,512]{1,0:T(8,128)(2,1)S(1)}, u32[]{:S(2)}) copy-start(bf16[3584,512]{1,0:T(8,128)(2,1)S(1)} %get-tuple-element.29) | copy-start | bytes 11010052
  104.9 66.0 %collective-permute-start = (bf16[1280,768]{1,0:T(8,128)(2,1)}, bf16[1280,768]{1,0:T(8,128)(2,1)}, u32[]{:S(2)}, u32[]{:S(2)}) collective-permute-start(bf16[1280,768]{1,0:T(8,128)(2,1)} %bitcast.6), channel_id=1, source_target_pairs={{0,32},{32,0},{64,96},{96,64},{128,160},{160,128},{192,224},{224,1... | collective-permute-start | bytes 5898248 | tf_op jit(solution)/shard_map/ppermute | solution.py:98
  160.5 5.6 %copy-start.3 = (bf16[3584,512]{1,0:T(8,128)(2,1)S(1)}, bf16[3584,512]{1,0:T(8,128)(2,1)}, u32[]{:S(2)}) copy-start(bf16[3584,512]{1,0:T(8,128)(2,1)} %copy-done.2) | copy-start | bytes 11010052
  171.0 3.3 copy-start.8
  174.2 3.5 %copy-start.1 = (bf16[512,3584]{1,0:T(8,128)(2,1)S(1)}, bf16[512,3584]{1,0:T(8,128)(2,1)}, u32[]{:S(2)}) copy-start(bf16[512,3584]{1,0:T(8,128)(2,1)} %fusion.5) | copy-start | bytes 11010052
  177.8 9.6 %copy-start.9 = (bf16[1280,512]{1,0:T(8,128)(2,1)}, bf16[1280,512]{1,0:T(8,128)(2,1)S(1)}, u32[]{:S(2)}) copy-start(bf16[1280,512]{1,0:T(8,128)(2,1)S(1)} %multiply_convert_fusion) | copy-start | bytes 3932164
  182.5 70.7 %all-to-all-start.5 = ((bf16[32,40,2048]{2,1,0:T(8,128)(2,1)}), bf16[32,40,2048]{2,1,0:T(8,128)(2,1)}, u32[]{:S(2)}, u32[]{:S(2)}) async-start(bf16[32,40,2048]{2,1,0:T(8,128)(2,1)} %bitcast.65), calls=%async_computation.5 | async-start | bytes 10485760 | tf_op jit(solution)/shard_map/all_to_all | solution.py:92
  187.3 136.9 %reduce-scatter.2.cloned.1.call-start = ((), (), s32[]{:S(2)}) async-start(), calls=%async_computation.8 | async-start | bytes 2359296 | tf_op jit(solution)/shard_map/reduce_scatter | solution.py:126
  191.0 70.9 %collective-permute-start.1 = (bf16[1280,768]{1,0:T(8,128)(2,1)}, bf16[1280,768]{1,0:T(8,128)(2,1)S(1)}, u32[]{:S(2)}, u32[]{:S(2)}) collective-permute-start(bf16[1280,768]{1,0:T(8,128)(2,1)} %convolution_convert_fusion.2), channel_id=1, source_target_pairs={{0,32},{32,0},{64,96},{96,64},{128,160},{160,128},{192,224},{224,1... | collective-permute-start | bytes 5898248 | tf_op jit(solution)/shard_map/ppermute | solution.py:118
  253.2 8.7 %copy-start.10 = (bf16[1280,512]{1,0:T(8,128)(2,1)S(1)}, bf16[1280,512]{1,0:T(8,128)(2,1)}, u32[]{:S(2)}) copy-start(bf16[1280,512]{1,0:T(8,128)(2,1)} %copy-done.9) | copy-start | bytes 3932164
Sparse Core Ops, SparseCore 0:
  22.6 45.1 all-gather.1
  262.0 35.1 reduce-scatter.1
where the time goes:
time: 335 us; the launch traced here: 333 us
  waiting for transfers between devices  154 us (46%)
  matrix products  61.2 us (18%)
  blocking collectives  55.9 us (17%)
  starting transfers between devices  26.2 us (8%)
  between operations  14.5 us (4%)
  other arithmetic  12.8 us (4%)
  local copies, waits for them, and re-layouts  8.04 us (2%)
    all_to_all x3, waiting for transfers between devices, exchange(): lax.all_to_all(rows.reshape(lane_count, block, -1), 'ex', split_axis=0, c...  120 us
    dot_general x13, matrix products, matmul(): return jnp.dot(a, b, preferred_element_type=jnp.float32)  61.2 us
    all_to_all x1, blocking collectives, exchange(): lax.all_to_all(rows.reshape(lane_count, block, -1), 'ex', split_axis=0, c...  30.1 us
    all_to_all x1, waiting for transfers between devices, shards(): lax.all_to_all(first, 'grp', split_axis=0, concat_axis=0, tiled=True)  27 us
    all_to_all x1, blocking collectives, shards(): lax.all_to_all(own_sums, 'grp', split_axis=0, concat_axis=0, tiled=True)  25.8 us
    all_to_all x3, starting transfers between devices, exchange(): lax.all_to_all(rows.reshape(lane_count, block, -1), 'ex', split_axis=0, c...  17.4 us
    select_n x2, other arithmetic, dequantize(): return jnp.where(is_hot, weights, scaled)  8.83 us
    all_to_all x1, starting transfers between devices, shards(): lax.all_to_all(first, 'grp', split_axis=0, concat_axis=0, tiled=True)  8.57 us
  transfers between devices with their start and end apart: 8, of which 5 were waited for; matrix products, arithmetic and copies ran while one was open for 19% of the time, Pallas kernels for 0%

commit v1 on v0

--- a/solution.py
+++ b/solution.py
@@ -1,12 +1,16 @@
 import jax
 import jax.numpy as jnp
 from jax import lax
+from jax.experimental import pallas as pl
+from jax.experimental.pallas import tpu as pltpu
 from jax.sharding import PartitionSpec as P
 
 
 CAP = 5
 HALF = 768
 BOTH = 2 * HALF
+HALF_BACK = 896
+BOTH_BACK = 2 * HALF_BACK
 
 
 def dequantize(weights, scales, is_hot):
@@ -20,12 +24,61 @@
     return jnp.dot(a, b, preferred_element_type=jnp.float32)
 
 
+def expert_kernel(
+    rows, gate_early, up_early, gate_matrix, up_matrix, down_rest, down_other, hidden, rest, other
+):
+    gate = gate_early[...] + matmul(rows[...], gate_matrix[...])
+    up = up_early[...] + matmul(rows[...], up_matrix[...])
+    hidden[...] = (gate / (1.0 + jnp.exp(-gate)) * up).astype(jnp.bfloat16)
+    other[...] = matmul(hidden[...], down_other[...]).astype(jnp.bfloat16)
+    rest[...] = matmul(hidden[...], down_rest[...]).astype(jnp.bfloat16)
+
+
+def expert_rest(rows, gate_early, up_early, gate_matrix, up_matrix, down_rest, down_other):
+    count, depth = rows.shape
+    units = gate_matrix.shape[1]
+    widths = [units, down_rest.shape[1], down_other.shape[1]]
+    width = sum(widths[1:])
+    tile = 256
+
+    def tiled(columns):
+        return pl.BlockSpec((tile, columns), lambda i: (i, 0))
+
+    def whole(array):
+        return pl.BlockSpec(array.shape, lambda i: (0, 0))
+
+    return pl.pallas_call(
+        expert_kernel,
+        grid=(count // tile,),
+        in_specs=[
+            tiled(depth),
+            tiled(units),
+            tiled(units),
+            whole(gate_matrix),
+            whole(up_matrix),
+            whole(down_rest),
+            whole(down_other),
+        ],
+        out_specs=[tiled(columns) for columns in widths],
+        out_shape=[jax.ShapeDtypeStruct((count, columns), jnp.bfloat16) for columns in widths],
+        compiler_params=pltpu.CompilerParams(
+            dimension_semantics=("arbitrary",)
+        ),
+        cost_estimate=pl.CostEstimate(
+            flops=2 * count * units * (2 * depth + width),
+            bytes_accessed=2 * (count * (depth + width + 5 * units) + units * (2 * depth + width)),
+            transcendentals=count * units,
+        ),
+        name="expert_rest",
+    )(rows, gate_early, up_early, gate_matrix, up_matrix, down_rest, down_other)
+
+
 def shards(
     tokens, expert_ids, combine, hot_flags, gate_up_weight, gate_up_scale, down_weight, down_scale
 ):
     group_count = lax.axis_size("grp")
     lane_count = lax.axis_size("ex")
-    token_count, _ = tokens.shape
+    token_count, model_width = tokens.shape
     top_count = expert_ids.shape[1]
     route_count = token_count * top_count
     block = group_count * CAP
@@ -33,8 +86,7 @@
     column_tokens = group_count * token_count
     own_grp = lax.axis_index("grp")
     own_pair = own_grp // 2
-    own_start = own_grp % 2 * HALF
-    other_start = HALF - own_start
+    parity = own_grp % 2
     partners = [(g, g ^ 1) for g in range(group_count)]
 
     flat_expert = expert_ids.reshape(route_count)
@@ -76,17 +128,32 @@
     slots_across = lax.broadcasted_iota(jnp.int32, (column_tokens, slot_count), 1)
     slot_t = slot.T
     pick = jnp.zeros((slot_count, column_tokens), jnp.bool_)
+    for k in range(top_count):
+        pick = pick | (slot_t[k][None, :] == slots_down)
+    pick = pick.astype(jnp.bfloat16)
     mix = jnp.zeros((column_tokens, slot_count), jnp.float32)
     for k in range(top_count):
-        pick = pick | (slot_t[k][None, :] == slots_down)
         mix = jnp.where(slot[:, k][:, None] == slots_across, weight[:, k][:, None], mix)
-    pick = pick.astype(jnp.bfloat16)
-    mix = mix.astype(jnp.bfloat16)
+    mix = lax.optimization_barrier(mix.astype(jnp.bfloat16))
 
     is_hot = hot_flags[own_pair * lane_count + lax.axis_index("ex")] == 1
-    gate_matrix = dequantize(gate_up_weight[0, 0, 0], gate_up_scale[0, 0, 0], is_hot)
-    up_matrix = dequantize(gate_up_weight[0, 0, 1], gate_up_scale[0, 0, 1], is_hot)
-    down_matrix = dequantize(down_weight[0, 0], down_scale[0, 0], is_hot)
+    group = model_width // gate_up_scale.shape[3]
+
+    def dequantize_gate_up(j, start, stop):
+        return dequantize(
+            gate_up_weight[0, 0, j, start:stop],
+            gate_up_scale[0, 0, j, start // group : stop // group],
+            is_hot,
+        )
+
+    first_matrices = [dequantize_gate_up(j, 0, BOTH) for j in range(2)]
+    rest_matrices = [dequantize_gate_up(j, BOTH, model_width) for j in range(2)]
+    down_first = dequantize(
+        down_weight[0, 0, :, :BOTH_BACK], down_scale[0, 0, :, :BOTH_BACK], is_hot
+    )
+    down_rest = dequantize(
+        down_weight[0, 0, :, BOTH_BACK:], down_scale[0, 0, :, BOTH_BACK:], is_hot
+    )
 
     def exchange(rows):
         return lax.all_to_all(
@@ -99,35 +166,34 @@
     rest_rows = matmul(pick, rest).astype(jnp.bfloat16)
     rest_rows = exchange(rest_rows)
 
-    def project(matrix):
-        return (
-            matmul(own_rows, lax.dynamic_slice_in_dim(matrix, own_start, HALF, 0))
-            + matmul(other_rows, lax.dynamic_slice_in_dim(matrix, other_start, HALF, 0))
-            + matmul(rest_rows, matrix[BOTH:])
-        )
-
-    gate = project(gate_matrix)
-    up = project(up_matrix)
-    hidden = (jax.nn.silu(gate) * up).astype(jnp.bfloat16)
-
-    rest_rows = matmul(hidden, down_matrix[:, BOTH:]).astype(jnp.bfloat16)
+    early = [
+        matmul(own_rows, lax.dynamic_slice_in_dim(matrix, parity * HALF, HALF, 0))
+        + matmul(other_rows, lax.dynamic_slice_in_dim(matrix, (1 - parity) * HALF, HALF, 0))
+        for matrix in first_matrices
+    ]
+    early = lax.optimization_barrier(early)
+    hidden, rest_rows, other_rows = expert_rest(
+        rest_rows,
+        *early,
+        *rest_matrices,
+        down_rest,
+        lax.dynamic_slice_in_dim(down_first, (1 - parity) * HALF_BACK, HALF_BACK, 1),
+    )
     rest_rows = exchange(rest_rows)
-    other_rows = matmul(
-        hidden, lax.dynamic_slice_in_dim(down_matrix, other_start, HALF, 1)
-    ).astype(jnp.bfloat16)
     partner_rows = lax.ppermute(other_rows, "grp", partners)
     own_rows = matmul(
-        hidden, lax.dynamic_slice_in_dim(down_matrix, own_start, HALF, 1)
+        hidden, lax.dynamic_slice_in_dim(down_first, parity * HALF_BACK, HALF_BACK, 1)
     ).astype(jnp.bfloat16)
+    own_rows = lax.optimization_barrier(own_rows)
     own_rows = own_rows.astype(jnp.float32) + partner_rows.astype(jnp.float32)
     own_rows = own_rows.astype(jnp.bfloat16)
     own_rows = exchange(own_rows)
     rest_sums = matmul(mix, rest_rows).astype(jnp.bfloat16)
     rest_out = lax.psum_scatter(rest_sums, "grp", scatter_dimension=0, tiled=True)
     own_sums = matmul(mix, own_rows).astype(jnp.bfloat16)
-    own_sums = own_sums.reshape(group_count, token_count, HALF)
+    own_sums = own_sums.reshape(group_count, token_count, HALF_BACK)
     sums = lax.all_to_all(own_sums, "grp", split_axis=0, concat_axis=0, tiled=True)
-    sums = sums.reshape(group_count // 2, 2, token_count, HALF).astype(jnp.float32)
+    sums = sums.reshape(group_count // 2, 2, token_count, HALF_BACK).astype(jnp.float32)
     sums = jnp.sum(sums, axis=0).astype(jnp.bfloat16)
     return jnp.concatenate([sums[0], sums[1], rest_out], axis=1)
 

time: 335 us -> 323 us (0.964)
  matrix products: 61.2 us -> 30.6 us
  blocking collectives: 55.9 us -> 31.8 us
  Pallas kernels: 0 us -> 15.7 us
  waiting for transfers between devices: 154 us -> 165 us
  other arithmetic: 12.8 us -> 21.1 us
  starting transfers between devices: 26.2 us -> 31.3 us
  local copies, waits for them, and re-layouts: 8.04 us -> 11.4 us
    all_to_all x3 -> x4, waiting for transfers between devices: 120 us -> 53 us  [exchange(): lax.all_to_all(rows.reshape(lane_count, block, -1), 'ex', split_axis=0, c...]
    ppermute x1, waiting for transfers between devices: 0.01 us -> 48 us  [shards(): partner_rows = lax.ppermute(other_rows, 'grp', partners)]
    dot_general x13 -> x9, matrix products: 61.2 us -> 30.6 us  [matmul(): return jnp.dot(a, b, preferred_element_type=jnp.float32)]
    all_to_all x1 -> x0, blocking collectives: 30.1 us -> none  [exchange(): lax.all_to_all(rows.reshape(lane_count, block, -1), 'ex', split_axis=0, c...]
    ppermute x1, waiting for transfers between devices: 0.01 us -> 29.9 us  [shards(): other_rows = lax.ppermute(own_rows, 'grp', partners)]
    pallas_call x0 -> x1, Pallas kernels: none -> 15.7 us  [expert_rest(): pl.pallas_call(expert_kernel, grid=(count // tile,), in_specs=[tiled(dept...]
    convert_element_type x0 -> x2, other arithmetic: none -> 6.97 us  [the longest x1 3.58 us: shards(): own_rows = own_rows.astype(jnp.bfloat16)]
    all_to_all x1, blocking collectives: 25.8 us -> 31.8 us  [shards(): lax.all_to_all(own_sums, 'grp', split_axis=0, concat_axis=0, tiled=True)]
  transfers between devices with their start and end apart: 8 -> 9, of which waited for: 5 -> 8; matrix products, arithmetic and copies ran while one was open for 19% -> 17% of each run, Pallas kernels for 0% -> 0%
where the time goes in v1:
time: 323 us; the launch traced here: 321 us
  waiting for transfers between devices  165 us (51%)
  blocking collectives  31.8 us (10%)
  starting transfers between devices  31.3 us (10%)
  matrix products  30.6 us (9%)
  other arithmetic  21.1 us (7%)
  Pallas kernels  15.7 us (5%)
  between operations  14.4 us (4%)
  local copies, waits for them, and re-layouts  11.4 us (4%)
    all_to_all x4, waiting for transfers between devices, exchange(): lax.all_to_all(rows.reshape(lane_count, block, -1), 'ex', split_axis=0, c...  53 us
    ppermute x1, waiting for transfers between devices, shards(): partner_rows = lax.ppermute(other_rows, 'grp', partners)  48 us
    all_to_all x1, blocking collectives, shards(): lax.all_to_all(own_sums, 'grp', split_axis=0, concat_axis=0, tiled=True)  31.8 us
    dot_general x9, matrix products, matmul(): return jnp.dot(a, b, preferred_element_type=jnp.float32)  30.6 us
    ppermute x1, waiting for transfers between devices, shards(): other_rows = lax.ppermute(own_rows, 'grp', partners)  29.9 us
    all_to_all x1, waiting for transfers between devices, shards(): lax.all_to_all(first, 'grp', split_axis=0, concat_axis=0, tiled=True)  27 us
    all_to_all x4, starting transfers between devices, exchange(): lax.all_to_all(rows.reshape(lane_count, block, -1), 'ex', split_axis=0, c...  22.1 us
    pallas_call x1, Pallas kernels, expert_rest(): pl.pallas_call(expert_kernel, grid=(count // tile,), in_specs=[tiled(dept...  15.7 us
  transfers between devices with their start and end apart: 9, of which 8 were waited for; matrix products, arithmetic and copies ran while one was open for 17% of the time, Pallas kernels for 0%

profile of v1, /device:TPU:32, one launch (start us, length us, event | category | flops | bytes accessed | tf_op | source)
XLA Modules:
  0.0 321.2 jit_solution(421724307191308645)
XLA Ops:
  11.5 8.6 %all-to-all-start = ((bf16[8,64,896]{2,1,0:T(8,128)(2,1)}), bf16[8,64,896]{2,1,0:T(8,128)(2,1)S(1)}, u32[]{:S(2)}, u32[]{:S(2)}) async-start(bf16[8,64,896]{2,1,0:T(8,128)(2,1)} %bitcast.2), calls=%async_computation | async-start | bytes 1835008 | tf_op jit(solution)/shard_map/all_to_all | solution.py:116
  20.8 27.0 %all-to-all-done = bf16[8,64,896]{2,1,0:T(8,128)(2,1)S(1)} async-done(((bf16[8,64,896]{2,1,0:T(8,128)(2,1)}), bf16[8,64,896]{2,1,0:T(8,128)(2,1)S(1)}, u32[]{:S(2)}, u32[]{:S(2)}) %all-to-all-start) | async-done | bytes 917536 | tf_op jit(solution)/shard_map/all_to_all | solution.py:116
  48.0 1.1 slice_reduce_fusion.7
  49.1 4.4 %convolution_convert_fusion.2 = bf16[1280,768]{1,0:T(8,128)(2,1)} fusion(bf16[512,896]{1,0:T(8,128)(2,1)S(1)} %bitcast.97, s32[512]{0:T(512)S(1)} %get-tuple-element.16, s32[512]{0:T(512)S(1)} %get-tuple-element.17, s32[512]{0:T(512)S(1)} %get-tuple-element.18, s32[512]{0:T(512)S(1)} %get-tuple-element.19, s32[512]{0:T(512)S(1)} %get-tuple-element.20, ...), kind=kOutput, calls=%fused_computation.13 | convolution fusion | flops 1017446400 | bytes 2768896 | tf_op jit(solution)/shard_map/dot_general | solution.py:24
  53.6 7.4 %all-to-all-start.2 = ((bf16[32,40,768]{2,1,0:T(8,128)(2,1)}), bf16[32,40,768]{2,1,0:T(8,128)(2,1)S(1)}, u32[]{:S(2)}, u32[]{:S(2)}) async-start(bf16[32,40,768]{2,1,0:T(8,128)(2,1)} %bitcast.104), calls=%async_computation.2 | async-start | bytes 3932160 | tf_op jit(solution)/shard_map/all_to_all | solution.py:159
  60.9 6.9 %all-gather.2.cloned.1.call-done = bf16[512,2048]{1,0:T(8,128)(2,1)} async-done(((bf16[64,2048]{1,0:T(8,128)(2,1)}), bf16[512,2048]{1,0:T(8,128)(2,1)}) %all-gather.2.cloned.1.call-update) | async-done | bytes 2097168 | tf_op jit(solution)/shard_map/all_gather | solution.py:118
  67.8 7.9 %convolution_convert_fusion = bf16[1280,2048]{1,0:T(8,128)(2,1)} fusion(bf16[512,2048]{1,0:T(8,128)(2,1)} %all-gather.2.cloned.1.call-done, s32[512]{0:T(512)S(1)} %get-tuple-element.16, s32[512]{0:T(512)S(1)} %get-tuple-element.17, s32[512]{0:T(512)S(1)} %get-tuple-element.18, s32[512]{0:T(512)S(1)} %get-tuple-element.19, s32[512]{0:T(512)S(1)} %get-tuple-element.20, ...), kind=kOutput, calls=%fused_computation | convolution fusion | flops 2696806400 | bytes 7356416 | tf_op jit(solution)/shard_map/dot_general | solution.py:24
  75.7 13.8 %all-to-all-done.2 = bf16[32,40,768]{2,1,0:T(8,128)(2,1)S(1)} async-done(((bf16[32,40,768]{2,1,0:T(8,128)(2,1)}), bf16[32,40,768]{2,1,0:T(8,128)(2,1)S(1)}, u32[]{:S(2)}, u32[]{:S(2)}) %all-to-all-start.2) | async-done | bytes 1966112 | tf_op jit(solution)/shard_map/all_to_all | solution.py:159
  89.4 1.3 copy-done.3
  90.7 4.9 %all-to-all-start.1 = ((bf16[32,40,2048]{2,1,0:T(8,128)(2,1)}), bf16[32,40,2048]{2,1,0:T(8,128)(2,1)}, u32[]{:S(2)}, u32[]{:S(2)}) async-start(bf16[32,40,2048]{2,1,0:T(8,128)(2,1)} %bitcast.93), calls=%async_computation.1 | async-start | bytes 10485760 | tf_op jit(solution)/shard_map/all_to_all | solution.py:159
  97.2 2.6 fusion.18
  99.9 5.3 %fusion.5 = (bf16[2048,512]{1,0:T(8,128)(2,1)}, bf16[2048,512]{1,0:T(8,128)(2,1)}) fusion(f32[16,512]{1,0:T(8,128)S(1)} %get-tuple-element.59, bf16[1,1,2,3584,512]{4,3,2,1,0:T(8,128)(2,1)} %param.12, pred[]{:T(512)} %bitcast.9, f32[16,512]{1,0:T(8,128)S(1)} %get-tuple-element.60), kind=kLoop, calls=%fused_computation.15 | loop fusion | flops 8388608 | bytes 8454145 | tf_op jit(solution)/shard_map/jit(_where)/select_n | solution.py:20
  105.3 2.2 fusion.9
  108.6 1.2 fusion.23
  109.8 1.2 fusion.26
  111.0 29.9 %collective-permute-done = bf16[1280,768]{1,0:T(8,128)(2,1)S(1)} collective-permute-done((bf16[1280,768]{1,0:T(8,128)(2,1)}, bf16[1280,768]{1,0:T(8,128)(2,1)S(1)}, u32[]{:S(2)}, u32[]{:S(2)}) %collective-permute-start) | collective-permute-done | bytes 1966112 | tf_op jit(solution)/shard_map/ppermute | solution.py:165
  140.9 2.7 convolution_add_fusion.up_early
  143.5 2.7 convolution_add_fusion.1.gate_early
  146.3 15.2 %all-to-all-done.1 = bf16[32,40,2048]{2,1,0:T(8,128)(2,1)} async-done(((bf16[32,40,2048]{2,1,0:T(8,128)(2,1)}), bf16[32,40,2048]{2,1,0:T(8,128)(2,1)}, u32[]{:S(2)}, u32[]{:S(2)}) %all-to-all-start.1) | async-done | bytes 5242912 | tf_op jit(solution)/shard_map/all_to_all | solution.py:159
  161.4 15.7 %expert_rest.1 = (bf16[1280,512]{1,0:T(8,128)(2,1)}, bf16[1280,1792]{1,0:T(8,128)(2,1)}, bf16[1280,896]{1,0:T(8,128)(2,1)}) custom-call(bf16[1280,2048]{1,0:T(8,128)(2,1)} %bitcast.6.rows, f32[1280,512]{1,0:T(8,128)} %convolution_add_fusion.1.gate_early, f32[1280,512]{1,0:T(8,128)} %convolution_add_fusion.up_early, ...), custom_call_target="tpu_custom_call" | custom-call | flops 8891924480 | bytes 25624576 | tf_op jit(solution)/shard_map/expert_rest/pallas_call | solution.py:50
  177.1 4.8 %all-to-all-start.5 = ((bf16[32,40,1792]{2,1,0:T(8,128)(2,1)}), bf16[32,40,1792]{2,1,0:T(8,128)(2,1)}, u32[]{:S(2)}, u32[]{:S(2)}) async-start(bf16[32,40,1792]{2,1,0:T(8,128)(2,1)} %bitcast.94), calls=%async_computation.5 | async-start | bytes 9175040 | tf_op jit(solution)/shard_map/all_to_all | solution.py:159
  184.9 1.5 convolution_convert_fusion.1
  186.4 48.0 %collective-permute-done.1 = bf16[1280,896]{1,0:T(8,128)(2,1)} collective-permute-done((bf16[1280,896]{1,0:T(8,128)(2,1)}, bf16[1280,896]{1,0:T(8,128)(2,1)}, u32[]{:S(2)}, u32[]{:S(2)}) %collective-permute-start.1) | collective-permute-done | bytes 2293792 | tf_op jit(solution)/shard_map/ppermute | solution.py:183
  234.5 3.6 %add_convert_fusion = bf16[1280,896]{1,0:T(8,128)(2,1)} fusion(bf16[1280,896]{1,0:T(8,128)(2,1)} %collective-permute-done.1, bf16[1280,896]{1,0:T(8,128)(2,1)S(1)} %convolution_convert_fusion.1), kind=kLoop, calls=%fused_computation.1 | loop fusion | flops 4587520 | bytes 6881280 | tf_op jit(solution)/shard_map/convert_element_type | solution.py:189
  238.0 2.3 all-to-all-done.5
  240.4 5.0 %all-to-all-start.3 = ((bf16[32,40,896]{2,1,0:T(8,128)(2,1)}), bf16[32,40,896]{2,1,0:T(8,128)(2,1)S(1)}, u32[]{:S(2)}, u32[]{:S(2)}) async-start(bf16[32,40,896]{2,1,0:T(8,128)(2,1)} %bitcast.28), calls=%async_computation.3 | async-start | bytes 4587520 | tf_op jit(solution)/shard_map/all_to_all | solution.py:159
  245.4 3.4 %select_convert_fusion = bf16[512,1280]{1,0:T(8,128)(2,1)S(1)} fusion(bf16[512]{0:T(512)(128)(2,1)S(1)} %get-tuple-element.32, s32[512]{0:T(512)S(1)} %get-tuple-element.24, bf16[512]{0:T(512)(128)(2,1)S(1)} %get-tuple-element.33, s32[512]{0:T(512)S(1)} %get-tuple-element.25, bf16[512]{0:T(512)(128)(2,1)S(1)} %get-tuple-element.34, ...), kind=kLoop, calls=%fused_computation.31 | loop fusion | flops 10485760 | bytes 1335296 | tf_op jit(solution)/shard_map/convert_element_type | solution.py:137
  249.9 6.1 %convolution_convert_fusion.3 = bf16[512,1792]{1,0:T(8,128)(2,1)} fusion(bf16[512,1280]{1,0:T(8,128)(2,1)S(1)} %select_convert_fusion, bf16[1280,1792]{1,0:T(8,128)(2,1)} %bitcast.35), kind=kOutput, calls=%fused_computation.20 | convolution fusion | flops 2349727744 | bytes 7733248 | tf_op jit(solution)/shard_map/dot_general | solution.py:24
  256.0 21.7 %all-to-all-done.3 = bf16[32,40,896]{2,1,0:T(8,128)(2,1)S(1)} async-done(((bf16[32,40,896]{2,1,0:T(8,128)(2,1)}), bf16[32,40,896]{2,1,0:T(8,128)(2,1)S(1)}, u32[]{:S(2)}, u32[]{:S(2)}) %all-to-all-start.3) | async-done | bytes 2293792 | tf_op jit(solution)/shard_map/all_to_all | solution.py:159
  277.8 2.8 convolution_convert_fusion.4
  280.6 31.8 %all_to_all.30 = bf16[8,64,896]{2,1,0:T(8,128)(2,1)S(1)} all-to-all(bf16[8,64,896]{2,1,0:T(8,128)(2,1)S(1)} %bitcast.105), channel_id=1, replica_groups=mesh['grp'=8,'ex'=32] {'grp'}, dimensions={0} | all-to-all | bytes 1835008 | tf_op jit(solution)/shard_map/all_to_all | solution.py:195
  312.6 1.7 pad_maximum_fusion
  (58 shorter events, 12.0 us)
Async XLA Ops:
  6.5 13.5 %copy-start.6 = (bf16[64,3584]{1,0:T(8,128)(2,1)S(1)}, bf16[64,3584]{1,0:T(8,128)(2,1)}, u32[]{:S(2)}) copy-start(bf16[64,3584]{1,0:T(8,128)(2,1)} %param.8) | copy-start | bytes 1376260
  11.5 36.3 %all-to-all-start = ((bf16[8,64,896]{2,1,0:T(8,128)(2,1)}), bf16[8,64,896]{2,1,0:T(8,128)(2,1)S(1)}, u32[]{:S(2)}, u32[]{:S(2)}) async-start(bf16[8,64,896]{2,1,0:T(8,128)(2,1)} %bitcast.2), calls=%async_computation | async-start | bytes 1835008 | tf_op jit(solution)/shard_map/all_to_all | solution.py:116
  20.0 47.8 %all-gather.2.cloned.1.call-start = ((), (), s32[]{:S(2)}) async-start(), calls=%async_computation.7 | async-start | bytes 2359296 | tf_op jit(solution)/shard_map/all_gather | solution.py:118
  53.6 35.9 %all-to-all-start.2 = ((bf16[32,40,768]{2,1,0:T(8,128)(2,1)}), bf16[32,40,768]{2,1,0:T(8,128)(2,1)S(1)}, u32[]{:S(2)}, u32[]{:S(2)}) async-start(bf16[32,40,768]{2,1,0:T(8,128)(2,1)} %bitcast.104), calls=%async_computation.2 | async-start | bytes 3932160 | tf_op jit(solution)/shard_map/all_to_all | solution.py:159
  89.4 1.3 copy-start.3
  89.4 6.4 %copy-start.7 = (f32[1,1,2,28,512]{4,2,3,1,0:T(2,128)S(1)}, f32[1,1,2,28,512]{4,2,3,1,0:T(2,128)}, u32[]{:S(2)}) copy-start(f32[1,1,2,28,512]{4,2,3,1,0:T(2,128)} %param.13) | copy-start | bytes 344068
  89.4 6.5 %copy-start.9 = (s32[128]{0:T(128)S(1)}, s32[128]{0:T(128)}, u32[]{:S(2)}) copy-start(s32[128]{0:T(128)} %param.11) | copy-start | bytes 1540
  90.7 70.7 %all-to-all-start.1 = ((bf16[32,40,2048]{2,1,0:T(8,128)(2,1)}), bf16[32,40,2048]{2,1,0:T(8,128)(2,1)}, u32[]{:S(2)}, u32[]{:S(2)}) async-start(bf16[32,40,2048]{2,1,0:T(8,128)(2,1)} %bitcast.93), calls=%async_computation.1 | async-start | bytes 10485760 | tf_op jit(solution)/shard_map/all_to_all | solution.py:159
  95.6 45.3 %collective-permute-start = (bf16[1280,768]{1,0:T(8,128)(2,1)}, bf16[1280,768]{1,0:T(8,128)(2,1)S(1)}, u32[]{:S(2)}, u32[]{:S(2)}) collective-permute-start(bf16[1280,768]{1,0:T(8,128)(2,1)} %bitcast.101), channel_id=1, source_target_pairs={{0,32},{32,0},{64,96},{96,64},{128,160},{160,128},{192,224},{224,1... | collective-permute-start | bytes 5898248 | tf_op jit(solution)/shard_map/ppermute | solution.py:165
  99.9 5.3 %copy-start.8 = (f32[1,1,4,3584]{3,2,1,0:T(4,128)S(1)}, f32[1,1,4,3584]{3,2,1,0:T(4,128)}, u32[]{:S(2)}) copy-start(f32[1,1,4,3584]{3,2,1,0:T(4,128)} %param.15) | copy-start | bytes 172036
  99.9 5.3 %copy-start.2 = (bf16[1,1,512,3584]{3,2,1,0:T(8,128)(2,1)S(1)}, bf16[1,1,512,3584]{3,2,1,0:T(8,128)(2,1)}, u32[]{:S(2)}) copy-start(bf16[1,1,512,3584]{3,2,1,0:T(8,128)(2,1)} %param.14) | copy-start | bytes 11010052
  105.3 3.3 %copy-start.4 = (bf16[32,40,768]{2,1,0:T(8,128)(2,1)S(1)}, bf16[32,40,768]{2,1,0:T(8,128)(2,1)}, u32[]{:S(2)}) copy-start(bf16[32,40,768]{2,1,0:T(8,128)(2,1)} %copy-done.3) | copy-start | bytes 5898244
  107.5 2.3 copy-start
  177.1 63.2 %all-to-all-start.5 = ((bf16[32,40,1792]{2,1,0:T(8,128)(2,1)}), bf16[32,40,1792]{2,1,0:T(8,128)(2,1)}, u32[]{:S(2)}, u32[]{:S(2)}) async-start(bf16[32,40,1792]{2,1,0:T(8,128)(2,1)} %bitcast.94), calls=%async_computation.5 | async-start | bytes 9175040 | tf_op jit(solution)/shard_map/all_to_all | solution.py:159
  182.0 2.9 copy-start.1
  182.0 52.5 %collective-permute-start.1 = (bf16[1280,896]{1,0:T(8,128)(2,1)}, bf16[1280,896]{1,0:T(8,128)(2,1)}, u32[]{:S(2)}, u32[]{:S(2)}) collective-permute-start(bf16[1280,896]{1,0:T(8,128)(2,1)} %get-tuple-element.13), channel_id=1, source_target_pairs={{0,32},{32,0},{64,96},{96,64},{128,160},{160,128},{192,224},{224,1... | collective-permute-start | bytes 6881288 | tf_op jit(solution)/shard_map/ppermute | solution.py:183
  182.3 2.6 copy-start.10
  240.4 37.4 %all-to-all-start.3 = ((bf16[32,40,896]{2,1,0:T(8,128)(2,1)}), bf16[32,40,896]{2,1,0:T(8,128)(2,1)S(1)}, u32[]{:S(2)}, u32[]{:S(2)}) async-start(bf16[32,40,896]{2,1,0:T(8,128)(2,1)} %bitcast.28), calls=%async_computation.3 | async-start | bytes 4587520 | tf_op jit(solution)/shard_map/all_to_all | solution.py:159
  245.4 67.2 %reduce-scatter.2.cloned.1.call-start = ((), (), s32[]{:S(2)}) async-start(), calls=%async_computation.8 | async-start | bytes 2064384 | tf_op jit(solution)/shard_map/reduce_scatter | solution.py:192
  248.8 1.1 copy-start.5
Sparse Core Ops, SparseCore 0:
  22.6 45.1 all-gather.1
  256.2 52.4 reduce-scatter.1

commit v2 on v1

--- a/solution.py
+++ b/solution.py
@@ -1,3 +1,5 @@
+import functools
+
 import jax
 import jax.numpy as jnp
 from jax import lax
@@ -73,6 +75,100 @@
     )(rows, gate_early, up_early, gate_matrix, up_matrix, down_rest, down_other)
 
 
+def pack_kernel(tokens, ids, weights, out):
+    top, count = ids.shape
+    experts = lax.broadcasted_iota(jnp.int32, (128, count), 0)
+    hits = [(experts == ids[k : k + 1, :]).astype(jnp.float32) for k in range(top)]
+    named = sum(hits).astype(jnp.bfloat16)
+    row = lax.broadcasted_iota(jnp.int32, (count, count), 0)
+    column = lax.broadcasted_iota(jnp.int32, (count, count), 1)
+    before = matmul(named, (row < column).astype(jnp.bfloat16))
+    ranks = [jnp.sum(hit * before, axis=0, keepdims=True) for hit in hits]
+    routes = jnp.concatenate(
+        [ids[...].astype(jnp.float32)]
+        + ranks
+        + [weights[...], jnp.zeros((128 - 3 * top, count), jnp.float32)],
+        axis=0,
+    ).astype(jnp.bfloat16)
+    routes = lax.dot_general(
+        (row == column).astype(jnp.bfloat16),
+        routes,
+        (((1,), (1,)), ((), ())),
+        preferred_element_type=jnp.float32,
+    ).astype(jnp.bfloat16)
+    for group in range(out.shape[0]):
+        start = group % 2 * HALF
+        out[group, :, :HALF] = tokens[:, start : start + HALF]
+        out[group, :, HALF:] = routes
+
+
+def pack(tokens, expert_ids, combine, group_count):
+    token_count, top_count = expert_ids.shape
+    whole = pl.BlockSpec((top_count, token_count), lambda i: (0, 0))
+    shape = (group_count, token_count, HALF + 128)
+    return pl.pallas_call(
+        pack_kernel,
+        grid=(1,),
+        in_specs=[pl.BlockSpec((token_count, BOTH), lambda i: (0, 0)), whole, whole],
+        out_specs=pl.BlockSpec(shape, lambda i: (0, 0, 0)),
+        out_shape=jax.ShapeDtypeStruct(shape, jnp.bfloat16),
+        name="pack",
+    )(tokens, expert_ids.T, combine.T)
+
+
+def pick_kernel(top, rank_count, pair, routes, tokens, out, slots):
+    tile = out.shape[0]
+    step = pl.program_id(0)
+
+    @pl.when(step == 0)
+    def _():
+        columns = routes.shape[1]
+        row = lax.broadcasted_iota(jnp.int32, (columns, columns), 0)
+        column = lax.broadcasted_iota(jnp.int32, (columns, columns), 1)
+        turned = lax.dot_general(
+            (row == column).astype(jnp.bfloat16),
+            routes[...],
+            (((1,), (1,)), ((), ())),
+            preferred_element_type=jnp.float32,
+        ).astype(jnp.int32)
+        block, lanes, source_tokens = rank_count * 8, 32, 64
+        source = lax.broadcasted_iota(jnp.int32, slots.shape, 1) // source_tokens
+        expert = turned[:top] - pair[0] * lanes
+        slots[...] = expert * block + source * rank_count + turned[top : 2 * top]
+
+    rows = lax.broadcasted_iota(jnp.int32, (tile, slots.shape[1]), 0) + step * tile
+    hit = rows == slots[0:1, :]
+    for k in range(1, top):
+        hit = hit | (rows == slots[k : k + 1, :])
+    out[...] = matmul(hit.astype(jnp.bfloat16), tokens[...]).astype(jnp.bfloat16)
+
+
+def pick(pair, first, tokens, width, slot_count, top_count):
+    count = first.shape[0]
+    tile = 256
+    return pl.pallas_call(
+        functools.partial(pick_kernel, top_count, CAP),
+        grid=(slot_count // tile,),
+        in_specs=[
+            pl.BlockSpec(memory_space=pltpu.SMEM),
+            pl.BlockSpec((count, 128), lambda i: (0, HALF // 128)),
+            pl.BlockSpec((count, width), lambda i: (0, 0)),
+        ],
+        out_specs=pl.BlockSpec((tile, width), lambda i: (i, 0)),
+        out_shape=pltpu.HBM((slot_count, width), jnp.bfloat16),
+        scratch_shapes=[pltpu.VMEM((top_count, count), jnp.int32)],
+        compiler_params=pltpu.CompilerParams(
+            dimension_semantics=("arbitrary",), vmem_limit_bytes=24 * 1024 * 1024
+        ),
+        cost_estimate=pl.CostEstimate(
+            flops=2 * slot_count * count * width,
+            bytes_accessed=2 * width * (slot_count + count),
+            transcendentals=0,
+        ),
+        name="pick",
+    )(pair[None], first, tokens)
+
+
 def shards(
     tokens, expert_ids, combine, hot_flags, gate_up_weight, gate_up_scale, down_weight, down_scale
 ):
@@ -80,7 +176,6 @@
     lane_count = lax.axis_size("ex")
     token_count, model_width = tokens.shape
     top_count = expert_ids.shape[1]
-    route_count = token_count * top_count
     block = group_count * CAP
     slot_count = lane_count * block
     column_tokens = group_count * token_count
@@ -89,30 +184,7 @@
     parity = own_grp % 2
     partners = [(g, g ^ 1) for g in range(group_count)]
 
-    flat_expert = expert_ids.reshape(route_count)
-    route_order = jnp.arange(route_count, dtype=jnp.int32)
-    earlier = (flat_expert[None, :] == flat_expert[:, None]) & (
-        route_order[None, :] < route_order[:, None]
-    )
-    route_rank = jnp.sum(earlier, axis=1, dtype=jnp.int32)
-
-    routes = jnp.concatenate(
-        [
-            expert_ids.astype(jnp.bfloat16),
-            route_rank.reshape(token_count, top_count).astype(jnp.bfloat16),
-            combine.astype(jnp.bfloat16),
-        ],
-        axis=1,
-    )
-    routes = jnp.pad(routes, ((0, 0), (0, 128 - 3 * top_count)))
-    first = jnp.stack(
-        [
-            jnp.concatenate([tokens[:, start : start + HALF], routes], axis=1)
-            for start in (0, HALF)
-        ]
-    )
-    first = jnp.broadcast_to(first[None], (group_count // 2,) + first.shape)
-    first = first.reshape(group_count, token_count, HALF + 128)
+    first = pack(tokens, expert_ids, combine, group_count)
     first = lax.all_to_all(first, "grp", split_axis=0, concat_axis=0, tiled=True)
     first = first.reshape(column_tokens, HALF + 128)
     rest = lax.all_gather(tokens[:, BOTH:], "grp", axis=0, tiled=True)
@@ -124,13 +196,7 @@
     source = jnp.arange(column_tokens, dtype=jnp.int32)[:, None] // token_count
     slot = (expert - own_pair * lane_count) * block + source * CAP + rank
 
-    slots_down = lax.broadcasted_iota(jnp.int32, (slot_count, column_tokens), 0)
     slots_across = lax.broadcasted_iota(jnp.int32, (column_tokens, slot_count), 1)
-    slot_t = slot.T
-    pick = jnp.zeros((slot_count, column_tokens), jnp.bool_)
-    for k in range(top_count):
-        pick = pick | (slot_t[k][None, :] == slots_down)
-    pick = pick.astype(jnp.bfloat16)
     mix = jnp.zeros((column_tokens, slot_count), jnp.float32)
     for k in range(top_count):
         mix = jnp.where(slot[:, k][:, None] == slots_across, weight[:, k][:, None], mix)
@@ -160,10 +226,12 @@
             rows.reshape(lane_count, block, -1), "ex", split_axis=0, concat_axis=0, tiled=True
         ).reshape(slot_count, -1)
 
-    own_rows = matmul(pick, first[:, :HALF]).astype(jnp.bfloat16)
+    own_rows = pick(own_pair, first, first, HALF, slot_count, top_count)
     own_rows = exchange(own_rows)
     other_rows = lax.ppermute(own_rows, "grp", partners)
-    rest_rows = matmul(pick, rest).astype(jnp.bfloat16)
+    rest_rows = pick(
+        own_pair, first, rest, model_width - BOTH, slot_count, top_count
+    )
     rest_rows = exchange(rest_rows)
 
     early = [

time: 323 us -> 325 us (level)
  Pallas kernels: 15.7 us -> 29.2 us
  matrix products: 30.6 us -> 18.2 us
  starting transfers between devices: 31.3 us -> 35.3 us
  other arithmetic: 21.1 us -> 17.6 us
    pallas_call x0 -> x3, Pallas kernels: none -> 13.6 us  [the longest x2 11.3 us: pick(): pl.pallas_call(functools.partial(pick_kernel, top_count, CAP), grid=(slot...]
    dot_general x9 -> x7, matrix products: 30.6 us -> 18.2 us  [matmul(): return jnp.dot(a, b, preferred_element_type=jnp.float32)]
    all_to_all x4, waiting for transfers between devices: 53 us -> 59 us  [exchange(): lax.all_to_all(rows.reshape(lane_count, block, -1), 'ex', split_axis=0, c...]
    all_gather x1, waiting for transfers between devices: 6.86 us -> 1.21 us  [shards(): rest = lax.all_gather(tokens[:, BOTH:], 'grp', axis=0, tiled=True)]
    all_to_all x1, waiting for transfers between devices: 27 us -> 32.5 us  [shards(): lax.all_to_all(first, 'grp', split_axis=0, concat_axis=0, tiled=True)]
  transfers between devices with their start and end apart: 9 -> 9, of which waited for: 8 -> 8; matrix products, arithmetic and copies ran while one was open for 17% -> 12% of each run, Pallas kernels for 0% -> 4%
where the time goes in v2:
time: 325 us; the launch traced here: 324 us
  waiting for transfers between devices  167 us (51%)
  starting transfers between devices  35.3 us (11%)
  blocking collectives  32.1 us (10%)
  Pallas kernels  29.2 us (9%)
  matrix products  18.2 us (6%)
  other arithmetic  17.6 us (5%)
  between operations  14.3 us (4%)
  local copies, waits for them, and re-layouts  9.67 us (3%)
    all_to_all x4, waiting for transfers between devices, exchange(): lax.all_to_all(rows.reshape(lane_count, block, -1), 'ex', split_axis=0, c...  59 us
    ppermute x1, waiting for transfers between devices, shards(): partner_rows = lax.ppermute(other_rows, 'grp', partners)  46.2 us
    all_to_all x1, waiting for transfers between devices, shards(): lax.all_to_all(first, 'grp', split_axis=0, concat_axis=0, tiled=True)  32.5 us
    all_to_all x1, blocking collectives, shards(): lax.all_to_all(own_sums, 'grp', split_axis=0, concat_axis=0, tiled=True)  32.1 us
    ppermute x1, waiting for transfers between devices, shards(): other_rows = lax.ppermute(own_rows, 'grp', partners)  28.2 us
    all_to_all x4, starting transfers between devices, exchange(): lax.all_to_all(rows.reshape(lane_count, block, -1), 'ex', split_axis=0, c...  21.4 us
    dot_general x7, matrix products, matmul(): return jnp.dot(a, b, preferred_element_type=jnp.float32)  18.2 us
    pallas_call x1, Pallas kernels, expert_rest(): pl.pallas_call(expert_kernel, grid=(count // tile,), in_specs=[tiled(dept...  15.7 us
  transfers between devices with their start and end apart: 9, of which 8 were waited for; matrix products, arithmetic and copies ran while one was open for 12% of the time, Pallas kernels for 4%

profile of v2, /device:TPU:32, one launch (start us, length us, event | category | flops | bytes accessed | tf_op | source)
XLA Modules:
  0.0 323.6 jit_solution(2467916847642025561)
XLA Ops:
  6.5 1.7 slice.125
  8.2 2.2 pack.1
  10.5 8.6 %all-to-all-start = ((bf16[8,64,896]{2,1,0:T(8,128)(2,1)}), bf16[8,64,896]{2,1,0:T(8,128)(2,1)S(1)}, u32[]{:S(2)}, u32[]{:S(2)}) async-start(bf16[8,64,896]{2,1,0:T(8,128)(2,1)} %pack.1), calls=%async_computation | async-start | bytes 1835008 | tf_op jit(solution)/shard_map/all_to_all | solution.py:188
  19.0 32.5 %all-to-all-done = bf16[8,64,896]{2,1,0:T(8,128)(2,1)S(1)} async-done(((bf16[8,64,896]{2,1,0:T(8,128)(2,1)}), bf16[8,64,896]{2,1,0:T(8,128)(2,1)S(1)}, u32[]{:S(2)}, u32[]{:S(2)}) %all-to-all-start) | async-done | bytes 917536 | tf_op jit(solution)/shard_map/all_to_all | solution.py:188
  51.5 4.9 %pick.3 = bf16[1280,768]{1,0:T(8,128)(2,1)} custom-call(s32[1]{0:T(128)} %bitcast.3.pair, bf16[512,896]{1,0:T(8,128)(2,1)S(1)} %bitcast.88, bf16[512,896]{1,0:T(8,128)(2,1)S(1)} %bitcast.89), custom_call_target="tpu_custom_call" | custom-call | flops 1006632960 | bytes 2752512 | tf_op jit(solution)/shard_map/pick/pallas_call | solution.py:149
  56.4 7.5 %all-to-all-start.2 = ((bf16[32,40,768]{2,1,0:T(8,128)(2,1)}), bf16[32,40,768]{2,1,0:T(8,128)(2,1)S(1)}, u32[]{:S(2)}, u32[]{:S(2)}) async-start(bf16[32,40,768]{2,1,0:T(8,128)(2,1)} %bitcast.93), calls=%async_computation.2 | async-start | bytes 3932160 | tf_op jit(solution)/shard_map/all_to_all | solution.py:225
  65.1 1.6 copy-done
  66.7 6.4 %pick.2 = bf16[1280,2048]{1,0:T(8,128)(2,1)} custom-call(s32[1]{0:T(128)} %bitcast.3.pair, bf16[512,896]{1,0:T(8,128)(2,1)S(1)} %bitcast.90, bf16[512,2048]{1,0:T(8,128)(2,1)S(1)} %copy-done), custom_call_target="tpu_custom_call" | custom-call | flops 2684354560 | bytes 7340032 | tf_op jit(solution)/shard_map/pick/pallas_call | solution.py:149
  73.1 19.3 %all-to-all-done.2 = bf16[32,40,768]{2,1,0:T(8,128)(2,1)S(1)} async-done(((bf16[32,40,768]{2,1,0:T(8,128)(2,1)}), bf16[32,40,768]{2,1,0:T(8,128)(2,1)S(1)}, u32[]{:S(2)}, u32[]{:S(2)}) %all-to-all-start.2) | async-done | bytes 1966112 | tf_op jit(solution)/shard_map/all_to_all | solution.py:225
  93.6 4.9 %all-to-all-start.1 = ((bf16[32,40,2048]{2,1,0:T(8,128)(2,1)}), bf16[32,40,2048]{2,1,0:T(8,128)(2,1)}, u32[]{:S(2)}, u32[]{:S(2)}) async-start(bf16[32,40,2048]{2,1,0:T(8,128)(2,1)} %bitcast.94), calls=%async_computation.1 | async-start | bytes 10485760 | tf_op jit(solution)/shard_map/all_to_all | solution.py:225
  98.5 2.6 collective-permute-start
  102.5 2.6 fusion.11
  105.2 5.3 %fusion.5 = (bf16[2048,512]{1,0:T(8,128)(2,1)}, bf16[2048,512]{1,0:T(8,128)(2,1)}) fusion(f32[16,512]{1,0:T(8,128)S(1)} %get-tuple-element.47, bf16[1,1,2,3584,512]{4,3,2,1,0:T(8,128)(2,1)} %param.12, pred[]{:T(512)} %bitcast.8, f32[16,512]{1,0:T(8,128)S(1)} %get-tuple-element.48), kind=kLoop, calls=%fused_computation.13 | loop fusion | flops 8388608 | bytes 8454145 | tf_op jit(solution)/shard_map/jit(_where)/select_n | solution.py:22
  110.5 2.2 fusion.9
  116.2 28.2 %collective-permute-done = bf16[1280,768]{1,0:T(8,128)(2,1)S(1)} collective-permute-done((bf16[1280,768]{1,0:T(8,128)(2,1)}, bf16[1280,768]{1,0:T(8,128)(2,1)S(1)}, u32[]{:S(2)}, u32[]{:S(2)}) %collective-permute-start) | collective-permute-done | bytes 1966112 | tf_op jit(solution)/shard_map/ppermute | solution.py:231
  144.4 2.7 convolution_add_fusion.up_early
  147.1 2.7 convolution_add_fusion.1.gate_early
  149.8 14.6 %all-to-all-done.1 = bf16[32,40,2048]{2,1,0:T(8,128)(2,1)} async-done(((bf16[32,40,2048]{2,1,0:T(8,128)(2,1)}), bf16[32,40,2048]{2,1,0:T(8,128)(2,1)}, u32[]{:S(2)}, u32[]{:S(2)}) %all-to-all-start.1) | async-done | bytes 5242912 | tf_op jit(solution)/shard_map/all_to_all | solution.py:225
  164.3 15.7 %expert_rest.1 = (bf16[1280,512]{1,0:T(8,128)(2,1)}, bf16[1280,1792]{1,0:T(8,128)(2,1)}, bf16[1280,896]{1,0:T(8,128)(2,1)}) custom-call(bf16[1280,2048]{1,0:T(8,128)(2,1)} %bitcast.5.rows, f32[1280,512]{1,0:T(8,128)} %convolution_add_fusion.1.gate_early, f32[1280,512]{1,0:T(8,128)} %convolution_add_fusion.up_early, ...), custom_call_target="tpu_custom_call" | custom-call | flops 8891924480 | bytes 25624576 | tf_op jit(solution)/shard_map/expert_rest/pallas_call | solution.py:52
  180.0 5.0 %all-to-all-start.5 = ((bf16[32,40,1792]{2,1,0:T(8,128)(2,1)}), bf16[32,40,1792]{2,1,0:T(8,128)(2,1)}, u32[]{:S(2)}, u32[]{:S(2)}) async-start(bf16[32,40,1792]{2,1,0:T(8,128)(2,1)} %bitcast.95), calls=%async_computation.5 | async-start | bytes 9175040 | tf_op jit(solution)/shard_map/all_to_all | solution.py:225
  185.1 2.6 collective-permute-start.1
  190.3 1.5 convolution_convert_fusion
  191.8 46.2 %collective-permute-done.1 = bf16[1280,896]{1,0:T(8,128)(2,1)S(1)} collective-permute-done((bf16[1280,896]{1,0:T(8,128)(2,1)}, bf16[1280,896]{1,0:T(8,128)(2,1)S(1)}, u32[]{:S(2)}, u32[]{:S(2)}) %collective-permute-start.1) | collective-permute-done | bytes 2293792 | tf_op jit(solution)/shard_map/ppermute | solution.py:251
  238.0 1.9 add_convert_fusion
  239.9 3.5 %all-to-all-done.5 = bf16[32,40,1792]{2,1,0:T(8,128)(2,1)} async-done(((bf16[32,40,1792]{2,1,0:T(8,128)(2,1)}), bf16[32,40,1792]{2,1,0:T(8,128)(2,1)}, u32[]{:S(2)}, u32[]{:S(2)}) %all-to-all-start.5) | async-done | bytes 4587552 | tf_op jit(solution)/shard_map/all_to_all | solution.py:225
  243.5 4.1 %all-to-all-start.3 = ((bf16[32,40,896]{2,1,0:T(8,128)(2,1)}), bf16[32,40,896]{2,1,0:T(8,128)(2,1)S(1)}, u32[]{:S(2)}, u32[]{:S(2)}) async-start(bf16[32,40,896]{2,1,0:T(8,128)(2,1)} %bitcast.27), calls=%async_computation.3 | async-start | bytes 4587520 | tf_op jit(solution)/shard_map/all_to_all | solution.py:225
  247.6 3.4 %select_convert_fusion = bf16[512,1280]{1,0:T(8,128)(2,1)S(1)} fusion(bf16[512]{0:T(512)(128)(2,1)S(1)} %get-tuple-element.24, s32[512]{0:T(512)S(1)} %get-tuple-element.16, bf16[512]{0:T(512)(128)(2,1)S(1)} %get-tuple-element.25, s32[512]{0:T(512)S(1)} %get-tuple-element.17, bf16[512]{0:T(512)(128)(2,1)S(1)} %get-tuple-element.26, ...), kind=kLoop, calls=%fused_computation.21 | loop fusion | flops 10485760 | bytes 1335296 | tf_op jit(solution)/shard_map/convert_element_type | solution.py:203
  252.0 6.1 %convolution_convert_fusion.1 = bf16[512,1792]{1,0:T(8,128)(2,1)} fusion(bf16[512,1280]{1,0:T(8,128)(2,1)S(1)} %select_convert_fusion, bf16[1280,1792]{1,0:T(8,128)(2,1)} %bitcast.34), kind=kOutput, calls=%fused_computation.18 | convolution fusion | flops 2349727744 | bytes 7733248 | tf_op jit(solution)/shard_map/dot_general | solution.py:26
  258.2 21.7 %all-to-all-done.3 = bf16[32,40,896]{2,1,0:T(8,128)(2,1)S(1)} async-done(((bf16[32,40,896]{2,1,0:T(8,128)(2,1)}), bf16[32,40,896]{2,1,0:T(8,128)(2,1)S(1)}, u32[]{:S(2)}, u32[]{:S(2)}) %all-to-all-start.3) | async-done | bytes 2293792 | tf_op jit(solution)/shard_map/all_to_all | solution.py:225
  279.9 2.8 convolution_convert_fusion.2
  282.7 32.1 %all_to_all.30 = bf16[8,64,896]{2,1,0:T(8,128)(2,1)S(1)} all-to-all(bf16[8,64,896]{2,1,0:T(8,128)(2,1)S(1)} %bitcast.101), channel_id=1, replica_groups=mesh['grp'=8,'ex'=32] {'grp'}, dimensions={0} | all-to-all | bytes 1835008 | tf_op jit(solution)/shard_map/all_to_all | solution.py:263
  315.1 1.7 pad_maximum_fusion
  (43 shorter events, 10.5 us)
Async XLA Ops:
  6.5 58.5 %all-gather.2.cloned.1.call-start = ((), (), s32[]{:S(2)}) async-start(), calls=%async_computation.7 | async-start | bytes 2359296 | tf_op jit(solution)/shard_map/all_gather | solution.py:190
  10.5 41.0 %all-to-all-start = ((bf16[8,64,896]{2,1,0:T(8,128)(2,1)}), bf16[8,64,896]{2,1,0:T(8,128)(2,1)S(1)}, u32[]{:S(2)}, u32[]{:S(2)}) async-start(bf16[8,64,896]{2,1,0:T(8,128)(2,1)} %pack.1), calls=%async_computation | async-start | bytes 1835008 | tf_op jit(solution)/shard_map/all_to_all | solution.py:188
  56.4 36.0 %all-to-all-start.2 = ((bf16[32,40,768]{2,1,0:T(8,128)(2,1)}), bf16[32,40,768]{2,1,0:T(8,128)(2,1)S(1)}, u32[]{:S(2)}, u32[]{:S(2)}) async-start(bf16[32,40,768]{2,1,0:T(8,128)(2,1)} %bitcast.93), calls=%async_computation.2 | async-start | bytes 3932160 | tf_op jit(solution)/shard_map/all_to_all | solution.py:225
  65.1 1.6 copy-start
  92.3 1.3 copy-start.4
  92.3 8.8 %copy-start.7 = (f32[1,1,2,28,512]{4,2,3,1,0:T(2,128)S(1)}, f32[1,1,2,28,512]{4,2,3,1,0:T(2,128)}, u32[]{:S(2)}) copy-start(f32[1,1,2,28,512]{4,2,3,1,0:T(2,128)} %param.13) | copy-start | bytes 344068
  92.3 8.8 %copy-start.9 = (s32[128]{0:T(128)S(1)}, s32[128]{0:T(128)}, u32[]{:S(2)}) copy-start(s32[128]{0:T(128)} %param.11) | copy-start | bytes 1540
  93.6 70.7 %all-to-all-start.1 = ((bf16[32,40,2048]{2,1,0:T(8,128)(2,1)}), bf16[32,40,2048]{2,1,0:T(8,128)(2,1)}, u32[]{:S(2)}, u32[]{:S(2)}) async-start(bf16[32,40,2048]{2,1,0:T(8,128)(2,1)} %bitcast.94), calls=%async_computation.1 | async-start | bytes 10485760 | tf_op jit(solution)/shard_map/all_to_all | solution.py:225
  98.5 45.9 %collective-permute-start = (bf16[1280,768]{1,0:T(8,128)(2,1)}, bf16[1280,768]{1,0:T(8,128)(2,1)S(1)}, u32[]{:S(2)}, u32[]{:S(2)}) collective-permute-start(bf16[1280,768]{1,0:T(8,128)(2,1)} %bitcast.98), channel_id=1, source_target_pairs={{0,32},{32,0},{64,96},{96,64},{128,160},{160,128},{192,224},{224,1... | collective-permute-start | bytes 5898248 | tf_op jit(solution)/shard_map/ppermute | solution.py:231
  105.1 5.3 %copy-start.8 = (f32[1,1,4,3584]{3,2,1,0:T(4,128)S(1)}, f32[1,1,4,3584]{3,2,1,0:T(4,128)}, u32[]{:S(2)}) copy-start(f32[1,1,4,3584]{3,2,1,0:T(4,128)} %param.15) | copy-start | bytes 172036
  105.2 5.3 %copy-start.3 = (bf16[1,1,512,3584]{3,2,1,0:T(8,128)(2,1)S(1)}, bf16[1,1,512,3584]{3,2,1,0:T(8,128)(2,1)}, u32[]{:S(2)}) copy-start(bf16[1,1,512,3584]{3,2,1,0:T(8,128)(2,1)} %param.14) | copy-start | bytes 11010052
  110.5 3.3 %copy-start.5 = (bf16[32,40,768]{2,1,0:T(8,128)(2,1)S(1)}, bf16[32,40,768]{2,1,0:T(8,128)(2,1)}, u32[]{:S(2)}) copy-start(bf16[32,40,768]{2,1,0:T(8,128)(2,1)} %copy-done.4) | copy-start | bytes 5898244
  112.7 2.3 copy-start.1
  180.0 63.4 %all-to-all-start.5 = ((bf16[32,40,1792]{2,1,0:T(8,128)(2,1)}), bf16[32,40,1792]{2,1,0:T(8,128)(2,1)}, u32[]{:S(2)}, u32[]{:S(2)}) async-start(bf16[32,40,1792]{2,1,0:T(8,128)(2,1)} %bitcast.95), calls=%async_computation.5 | async-start | bytes 9175040 | tf_op jit(solution)/shard_map/all_to_all | solution.py:225
  185.1 52.9 %collective-permute-start.1 = (bf16[1280,896]{1,0:T(8,128)(2,1)}, bf16[1280,896]{1,0:T(8,128)(2,1)S(1)}, u32[]{:S(2)}, u32[]{:S(2)}) collective-permute-start(bf16[1280,896]{1,0:T(8,128)(2,1)} %get-tuple-element.13), channel_id=1, source_target_pairs={{0,32},{32,0},{64,96},{96,64},{128,160},{160,128},{192,224},{224,1... | collective-permute-start | bytes 6881288 | tf_op jit(solution)/shard_map/ppermute | solution.py:251
  187.9 2.4 copy-start.2
  187.9 2.4 copy-start.10
  243.5 36.4 %all-to-all-start.3 = ((bf16[32,40,896]{2,1,0:T(8,128)(2,1)}), bf16[32,40,896]{2,1,0:T(8,128)(2,1)S(1)}, u32[]{:S(2)}, u32[]{:S(2)}) async-start(bf16[32,40,896]{2,1,0:T(8,128)(2,1)} %bitcast.27), calls=%async_computation.3 | async-start | bytes 4587520 | tf_op jit(solution)/shard_map/all_to_all | solution.py:225
  247.5 67.5 %reduce-scatter.2.cloned.1.call-start = ((), (), s32[]{:S(2)}) async-start(), calls=%async_computation.8 | async-start | bytes 2064384 | tf_op jit(solution)/shard_map/reduce_scatter | solution.py:260
  251.0 1.1 copy-start.6
Sparse Core Ops, SparseCore 0:
  9.1 55.8 all-gather.1
  258.3 49.2 reduce-scatter.1
